TPU v7x, 32 devices: a whole 2x2x4 slice. The times are simulated.
32 devices in a mesh: section: 16 (over z, y, core), walk: 2 (over x).
Axes of the slice: x: 2, y: 2, z: 4, core: 2. Of those that a mesh axis runs over, the one named last changes fastest.
Arguments:
- fields: bfloat16 [16, 8, 800], P('section', None, 'walk'), may hold values from -4 to 4
- cholesky_vectors: bfloat16 [800, 200, 200], P('walk'), may hold values from -0.013 to 0.013
- trial_state: float32 [200, 100], replicated, may hold values from -1.6 to 1.6
- deviation: bfloat16 [16, 8, 200, 100], P('section', 'walk'), may hold values from -0.1796875 to 0.1796875
Outputs:
- density: float32 [8, 200, 200], P('walk')
All inputs are finite; a program needn't handle non-finite values.
Results may differ from a plain program's by a relative error of at most 0.0003.
Values sent between devices are 32-bit elements; how exact they have to be, the bound alone decides.
A program may use at most 128 MiB of HBM per device.

v0:
```python
import jax
import jax.numpy as jnp
from jax import lax
from jax.sharding import PartitionSpec as P

TAYLOR = 6


exact_mode = lax.Precision.HIGHEST


def entering(shard, axis, combine, identity):
    size, position = (lax.axis_size(axis), lax.axis_index(axis))
    everything = lax.all_gather(shard, axis)
    start = jnp.broadcast_to(jnp.asarray(identity, shard.dtype), shard.shape)

    def lap(k, before):
        at = size - 1 - k
        reached = at > position
        new = combine(before, everything[at])
        return jnp.where(reached, new, before)

    return lax.fori_loop(0, size, lap, start)


def series_matrix(field_matrix):
    orbitals = field_matrix.shape[-1]
    series_term = jnp.broadcast_to(jnp.eye(orbitals, dtype=jnp.float32), field_matrix.shape)
    summed = series_term
    for degree in range(1, TAYLOR + 1):
        series_term = (
            jnp.einsum("wij,wjk->wik", series_term, field_matrix, precision=exact_mode) / degree
        )
        summed = summed + series_term
    return summed


def solve_normal(factor, right_side):
    return jax.scipy.linalg.cho_solve((factor, True), right_side)


def green_block(left_state, walker):
    intersection = jnp.einsum("wie,wif->wef", left_state, walker, precision=exact_mode)
    normal_matrix = jnp.einsum("wef,weg->wfg", intersection, intersection, precision=exact_mode)
    right_side = jnp.einsum("wef,wie->wfi", intersection, left_state, precision=exact_mode)
    factor = jnp.linalg.cholesky(normal_matrix)
    solved = jax.vmap(solve_normal)(factor, right_side)
    return jnp.einsum("wie,wej->wij", walker, solved, precision=exact_mode)


def body(fields, cholesky_vectors, trial_state, deviation):
    steps_here, walker_count, chol_here = fields.shape
    orbitals = cholesky_vectors.shape[1]
    per_device = deviation.shape[1]
    field_rows = jnp.swapaxes(fields, 0, 1).reshape(walker_count * steps_here, chol_here)
    vector_table = cholesky_vectors.reshape(chol_here, orbitals * orbitals)
    field_matrices = lax.psum_scatter(
        jnp.dot(field_rows, vector_table, preferred_element_type=jnp.float32),
        "walk",
        scatter_dimension=0,
        tiled=True,
    )
    field_matrices = field_matrices.reshape(per_device, steps_here, orbitals, orbitals)
    walkers = trial_state + deviation.astype(jnp.float32)
    section_count = lax.axis_size("section")
    total_steps = steps_here * section_count
    series = [series_matrix(field_matrices[:, 0])]
    identity = jnp.broadcast_to(
        jnp.eye(orbitals, dtype=jnp.float32), (per_device, orbitals, orbitals)
    )
    block_map = identity
    for offset in reversed(range(steps_here)):
        block_map = jnp.einsum("wji,wjk->wik", series[offset], block_map, precision=exact_mode)

    def compose(earlier, later):
        return jnp.einsum("wij,wjk->wik", later, earlier, precision=exact_mode)

    prefix = entering(block_map, "section", compose, identity)
    incoming = jnp.einsum("wij,je->wie", prefix, trial_state, precision=exact_mode)
    left_state = incoming
    running = jnp.zeros((incoming.shape[0], orbitals, orbitals), jnp.float32)
    for offset in reversed(range(steps_here)):
        left_state = jnp.einsum("wji,wje->wie", series[offset], left_state, precision=exact_mode)
        running = running + green_block(left_state, walkers[offset])
    running, leaving = (running, left_state)
    summed = lax.psum(running, "section")
    return summed / total_steps


def solution(mesh):
    in_specs = (
        P("section", None, "walk"),
        P("walk", None, None),
        P(),
        P("section", "walk", None, None),
    )
    out_specs = P("walk", None, None)
    return jax.shard_map(body, mesh=mesh, in_specs=in_specs, out_specs=out_specs, check_vma=False)
```

profile of v0, /device:TPU:0, one launch (start us, length us, event | category | flops | bytes accessed | tf_op | source)
XLA Modules:
  0.0 450.3 jit_solution(12506095595911162128)
XLA Ops:
  6.5 57.5 %reshape.20 = bf16[400,40000]{1,0:T(8,128)(2,1)} reshape(bf16[400,200,200]{2,1,0:T(8,128)(2,1)} %param.7) | data formatting | bytes 64000000 | tf_op jit(solution)/shard_map/reshape | solution.py:56
  64.0 13.4 %fusion.22 = f32[8,40000]{1,0:T(8,128)} fusion(bf16[400,40000]{1,0:T(8,128)(2,1)} %reshape.20, bf16[1,8,400]{2,1,0:T(8,128)(2,1)S(1)} %copy-done), kind=kOutput, calls=%fused_computation.36 | convolution fusion | flops 256000000 | bytes 33286400 | tf_op jit(solution)/shard_map/dot_general | solution.py:58
  78.8 46.8 %all-reduce.6.cloned.1.call-done = f32[8,40000]{1,0:T(8,128)} async-done(((f32[8,40000]{1,0:T(8,128)}), f32[8,40000]{1,0:T(8,128)}) %all-reduce.6.cloned.1.call-update) | async-done | bytes 1280016
  133.5 2.6 fusion.8
  136.4 103.8 %all-gather.3.cloned.1.call-done = f32[64,200,200]{2,1,0:T(8,128)} async-done(((f32[4,200,200]{2,1,0:T(8,128)}), f32[64,200,200]{2,1,0:T(8,128)}) %all-gather.3.cloned.1.call-update) | async-done | bytes 10240016 | tf_op jit(solution)/shard_map/all_gather | solution.py:14
  240.2 34.8 %while.15 = (s32[]{:T(128)}, f32[4,200,200]{2,1,0:T(8,128)S(1)}, s32[]{:T(128)}, f32[16,4,200,200]{3,2,1,0:T(8,128)}, s32[]{:T(128)}, /*index=5*/s32[]{:T(128)}, s32[]{:T(128)}, s32[]{:T(128)}) while((s32[]{:T(128)}, f32[4,200,200]{2,1,0:T(8,128)S(1)}, s32[]{:T(128)}, f32[16,4,200,200]{3,2,1,0:T(8,128)}, s32[]{:T(128)}, /*index=5*/s32[]{:T(128)}, ...), condition=%wide.region_2.3_spmd, body=%wide.region_1.2_spmd.sunk | while | flops 384160000 | bytes 4377745 | solution.py:23
  240.3 2.1 convolution_select_fusion.2
  242.5 2.1 convolution_select_fusion.2
  244.7 2.1 convolution_select_fusion.2
  246.8 2.1 convolution_select_fusion.2
  249.0 2.1 convolution_select_fusion.2
  251.2 2.1 convolution_select_fusion.2
  253.3 2.1 convolution_select_fusion.2
  255.5 2.1 convolution_select_fusion.2
  257.7 2.1 convolution_select_fusion.2
  259.9 2.1 convolution_select_fusion.2
  262.0 2.1 convolution_select_fusion.2
  264.2 2.1 convolution_select_fusion.2
  266.4 2.1 convolution_select_fusion.2
  268.6 2.1 convolution_select_fusion.2
  280.0 36.7 %custom-call.11 = f32[4,100,100]{2,1,0:T(8,128)S(1)} custom-call(f32[4,100,100]{2,1,0:T(8,128)S(1)} %fusion.16), custom_call_target="Cholesky" | custom-call | tf_op jit(solution)/shard_map/jit(cholesky)/cholesky | solution.py:46
  317.0 31.0 %custom-call.12 = f32[4,1,100,100]{2,3,1,0:T(8,128)S(1)} custom-call(f32[4,1,100,100]{3,2,1,0:T(8,128)S(1)} %select_bitcast_fusion), custom_call_target="InvertDiagBlocksLowerTriangular" | custom-call | tf_op jit(solution)/shard_map/vmap(jit(_cho_solve))/triangular_solve | solution.py:39
  351.3 90.3 %all-reduce.4.cloned.1.call-done = f32[4,200,200]{2,1,0:T(8,128)} async-done(((f32[4,200,200]{2,1,0:T(8,128)}), f32[4,200,200]{2,1,0:T(8,128)}) %all-reduce.4.cloned.1.call-update) | async-done | bytes 640016 | tf_op jit(solution)/shard_map/psum | solution.py:86
  441.7 2.1 broadcast_multiply_fusion
  (58 shorter events, 22.5 us)
Async XLA Ops:
  6.5 57.5 %copy-start = (bf16[1,8,400]{2,1,0:T(8,128)(2,1)S(1)}, bf16[1,8,400]{2,1,0:T(8,128)(2,1)}, u32[]{:S(2)}) copy-start(bf16[1,8,400]{2,1,0:T(8,128)(2,1)} %param.6) | copy-start | bytes 19204
  6.5 119.0 %all-reduce.6.cloned.1.call-start = ((), (), s32[]{:S(2)}) async-start(), calls=%async_computation.2 | async-start | bytes 2564096
  64.0 13.5 %copy-start.3 = (u32[32]{0:T(128)S(1)}, u32[32]{0:T(128)}, u32[]{:S(2)}) copy-start(u32[32]{0:T(128)} %constant.123) | copy-start | bytes 388
  77.4 162.7 %all-gather.3.cloned.1.call-start = ((), (), s32[]{:S(2)}) async-start(), calls=%async_computation.1 | async-start | bytes 13926400 | tf_op jit(solution)/shard_map/all_gather | solution.py:14
  133.4 141.6 %copy-start.1 = (f32[200,100]{1,0:T(8,128)S(1)}, f32[200,100]{1,0:T(8,128)}, u32[]{:S(2)}) copy-start(f32[200,100]{1,0:T(8,128)} %param.8) | copy-start | bytes 240004
  136.1 141.5 %copy-start.2 = (bf16[1,4,200,100]{3,2,1,0:T(8,128)(2,1)S(1)}, bf16[1,4,200,100]{3,2,1,0:T(8,128)(2,1)}, u32[]{:S(2)}) copy-start(bf16[1,4,200,100]{3,2,1,0:T(8,128)(2,1)} %param.9) | copy-start | bytes 480004
  136.1 305.6 %all-reduce.4.cloned.1.call-start = ((), (), s32[]{:S(2)}) async-start(), calls=%async_computation | async-start | bytes 1638400 | tf_op jit(solution)/shard_map/psum | solution.py:86
Sparse Core Ops, SparseCore 0:
  77.6 47.9 all-reduce.5
  136.2 103.9 all-gather.2
  351.5 90.1 all-reduce.3
where the time goes:
time: 453 us; the launch traced here: 450 us
  waiting for transfers between devices  241 us (53%)
  other arithmetic  70.1 us (15%)
  matrix products  63.1 us (14%)
  local copies, waits for them, and re-layouts  61.3 us (14%)
  between operations  14 us (3%)
    all_gather x1, waiting for transfers between devices, entering(): everything = lax.all_gather(shard, axis)  104 us
    psum x1, waiting for transfers between devices, body(): summed = lax.psum(running, 'section')  90.3 us
    reshape x1, local copies, waits for them, and re-layouts, body(): vector_table = cholesky_vectors.reshape(chol_here, orbitals * orbitals)  57.5 us
    unnamed x4, waiting for transfers between devices  46.8 us
    another operation x4, other arithmetic, green_block(): factor = jnp.linalg.cholesky(normal_matrix)  36.9 us
    dot_general x16, matrix products, compose(): return jnp.einsum('wij,wjk->wik', later, earlier, precision=exact_mode)  33.2 us
    another operation x3, other arithmetic, solve_normal(): return jax.scipy.linalg.cho_solve((factor, True), right_side)  31.1 us
    dot_general x1, matrix products, body(): jnp.dot(field_rows, vector_table, preferred_element_type=jnp.float32)  13.4 us
  transfers between devices with their start and end apart: 3, of which 3 were waited for; matrix products, arithmetic and copies ran while one was open for 0% of the time, Pallas kernels for 0%

commit v1 on v0

v1 whole, which is shorter than its diff:
```python
import functools
import math

import jax
import jax.numpy as jnp
from jax import lax
from jax.experimental import pallas as pl
from jax.experimental.pallas import tpu as pltpu
from jax.sharding import Mesh, PartitionSpec as P

PACK = 16
SUB = 8


def split(a):
    high = a.astype(jnp.bfloat16)
    return high, (a - high.astype(jnp.float32)).astype(jnp.bfloat16)


def dot_f32(a, b):
    return jnp.dot(a, b, preferred_element_type=jnp.float32)


def dot3(a, b):
    a_high, a_low = split(a)
    b_high, b_low = split(b)
    return dot_f32(a_high, b_high) + (dot_f32(a_high, b_low) + dot_f32(a_low, b_high))


def contract_kernel(orbitals, field_ref, table_ref, out_ref, factor_ref):
    block = pl.program_id(0)
    rows, depth = field_ref.shape[1], field_ref.shape[2]
    low_part = (block * PACK) // orbitals
    high_part = (block * PACK + SUB) // orbitals
    changed = (
        (block == 0)
        | (low_part != ((block - 1) * PACK) // orbitals)
        | (high_part != ((block - 1) * PACK + SUB) // orbitals)
    )

    @pl.when(block == 0)
    def _():
        out_ref[...] = jnp.zeros_like(out_ref)

    @pl.when(changed)
    def _():
        sub = lax.broadcasted_iota(jnp.int32, (PACK, depth), 0)
        lane = lax.broadcasted_iota(jnp.int32, (PACK, depth), 1) % PACK
        for row in range(rows):
            low = field_ref[low_part, pl.ds(row, 1), :]
            high = field_ref[high_part, pl.ds(row, 1), :]
            value = jnp.where(sub < SUB, low, high)
            factor_ref[row * PACK : (row + 1) * PACK, :] = jnp.where(
                sub == lane, value, 0.0
            ).astype(jnp.bfloat16)

    table = table_ref[...].reshape(depth, orbitals)
    product = dot_f32(factor_ref[...], table).reshape(rows, PACK, orbitals)
    bands = orbitals // SUB
    for half in range(PACK // SUB):
        at = pl.multiple_of(((2 * block + half) % bands) * SUB, SUB)
        out_ref[:, pl.ds(at, SUB), :] += product[:, half * SUB : (half + 1) * SUB, :]


def contract(field_rows, cholesky_vectors):
    rows, chol = field_rows.shape
    orbitals = cholesky_vectors.shape[1]
    group = PACK // math.gcd(PACK, orbitals)
    supers = chol // group
    blocks = group * orbitals // PACK
    depth = supers * PACK
    field = field_rows.astype(jnp.float32).reshape(rows, supers, group)
    field = jnp.repeat(jnp.transpose(field, (2, 0, 1)), PACK, axis=2)
    table = cholesky_vectors.reshape(supers, blocks, PACK, orbitals)
    return pl.pallas_call(
        functools.partial(contract_kernel, orbitals),
        grid=(blocks,),
        in_specs=[
            pl.BlockSpec((group, rows, depth), lambda b: (0, 0, 0)),
            pl.BlockSpec((supers, None, PACK, orbitals), lambda b: (0, b, 0, 0)),
        ],
        out_specs=pl.BlockSpec((rows, orbitals, orbitals), lambda b: (0, 0, 0)),
        out_shape=jax.ShapeDtypeStruct((rows, orbitals, orbitals), jnp.float32),
        scratch_shapes=[pltpu.VMEM((rows * PACK, depth), jnp.bfloat16)],
        compiler_params=pltpu.CompilerParams(vmem_limit_bytes=56 * 2**20),
    )(field, table)


def eye(size):
    row = lax.broadcasted_iota(jnp.int32, (size, size), 0)
    column = lax.broadcasted_iota(jnp.int32, (size, size), 1)
    return jnp.where(row == column, 1.0, 0.0)


def series_kernel(place_ref, field_ref, keep_ref, give_ref):
    core = place_ref[1]
    half, orbitals = keep_ref.shape[0], keep_ref.shape[1]
    unit = eye(orbitals)

    def series(v):
        v2 = dot3(v, v)
        v3 = dot3(v2, v)
        upper = unit * (1 / 6) + v * (1 / 24) + v2 * (1 / 120) + v3 * (1 / 720)
        return (unit + v + v2 * 0.5) + dot3(v3, upper)

    for j in range(half):
        keep_ref[j] = series(field_ref[core * half + j])
        give_ref[j] = series(field_ref[(1 - core) * half + j])


def pair_kernel(place_ref, keep_ref, other_ref, out_ref):
    core = place_ref[1]
    for j in range(keep_ref.shape[0]):
        keep, other = keep_ref[j], other_ref[j]
        later = jnp.where(core == 0, other, keep)
        earlier = jnp.where(core == 0, keep, other)
        out_ref[j] = dot3(later, earlier)


def green_kernel(
    scale, place_ref, all_ref, keep_ref, other_ref, trial_ref, walk_ref, walk_other_ref,
    out_ref, left_ref, inter_ref, inverse_ref,
):
    chip, core = place_ref[0], place_ref[1]
    chips, half = all_ref.shape[0], all_ref.shape[1]
    electrons = trial_ref.shape[0]

    for j in range(half):
        left_ref[j] = trial_ref[...]

    def lap(k, _):
        for j in range(half):
            left_ref[j] = dot3(left_ref[j], all_ref[chips - 1 - k, j])
        return 0

    lax.fori_loop(0, chips - 1 - chip, lap, 0)
    unit = eye(electrons)

    def walker(j, step):
        mine = core == step
        return jnp.where(mine, walk_ref[j], walk_other_ref[j])

    for j in range(half):
        keep, other = keep_ref[j], other_ref[j]
        later = jnp.where(core == 0, other, keep)
        earlier = jnp.where(core == 0, keep, other)
        after_late = dot3(left_ref[j], later)
        left_ref[half + j] = after_late
        left_ref[j] = dot3(after_late, earlier)
    for step in range(2):
        for j in range(half):
            at = step * half + j
            inter = dot3(left_ref[at], walker(j, step))
            inter_ref[at] = inter
            flipped = inter.T
            square = dot3(inter, flipped)
            inverse_ref[at] = flipped * lax.rsqrt(jnp.sum(square * square))

    def newton():
        worst = jnp.float32(0.0)
        for at in range(2 * half):
            guess = inverse_ref[at]
            rest = unit - dot3(inter_ref[at], guess)
            inverse_ref[at] = guess + dot3(guess, rest)
            worst = jnp.maximum(worst, jnp.sum(rest * rest))
        return worst

    def going(state):
        return (state[0] < 80) & (state[1] > 1e-4)

    lax.while_loop(going, lambda state: (state[0] + 1, newton()), (jnp.int32(0), jnp.float32(1.0)))
    newton()
    for j in range(half):
        total = None
        for step in range(2):
            at = step * half + j
            green = dot3(walker(j, step), dot3(inverse_ref[at], left_ref[at]))
            total = green if total is None else total + green
        out_ref[j] = total * scale


def call(kernel, out_shapes, args, scratch=()):
    vmem = pl.BlockSpec(memory_space=pltpu.VMEM)
    return pl.pallas_call(
        kernel,
        in_specs=[pl.BlockSpec(memory_space=pltpu.SMEM)] + [vmem] * (len(args) - 1),
        out_specs=jax.tree.map(lambda _: vmem, out_shapes),
        out_shape=out_shapes,
        scratch_shapes=list(scratch),
        compiler_params=pltpu.CompilerParams(vmem_limit_bytes=48 * 2**20),
    )(*args)


def body(fields, cholesky_vectors, trial_state, deviation):
    chol = fields.shape[2]
    orbitals, electrons = trial_state.shape
    per_device = deviation.shape[1]
    half = per_device // 2
    chips = lax.axis_size("chip")
    chip, core = lax.axis_index("chip"), lax.axis_index("core")
    walk_size, walk = lax.axis_size("walk"), lax.axis_index("walk")
    place = jnp.stack([chip, core]).astype(jnp.int32)
    swap = [(0, 1), (1, 0)]

    def half_of(array, which):
        return lax.dynamic_slice_in_dim(array, which * half, half, 0)

    walkers = trial_state + deviation[0].astype(jnp.float32)
    walkers_keep = half_of(walkers, core)
    walkers_other = lax.ppermute(half_of(walkers, 1 - core), "core", swap)

    partial = contract(fields.reshape(-1, chol), cholesky_vectors)

    def owned(device):
        return lax.dynamic_slice_in_dim(partial, device * per_device, per_device, 0)

    field_matrix = owned(walk)
    for shift in range(1, walk_size):
        ring = [(i, (i + shift) % walk_size) for i in range(walk_size)]
        field_matrix = field_matrix + lax.ppermute(
            owned((walk + shift) % walk_size), "walk", ring
        )

    square = jax.ShapeDtypeStruct((half, orbitals, orbitals), jnp.float32)
    keep, give = call(series_kernel, (square, square), (place, field_matrix))
    other = lax.ppermute(give, "core", swap)
    pair = call(pair_kernel, square, (place, keep, other))
    everything = lax.all_gather(pair, "chip")
    density = call(
        functools.partial(green_kernel, 1.0 / (2 * chips)),
        square,
        (place, everything, keep, other, trial_state.T, walkers_keep, walkers_other),
        [
            pltpu.VMEM((2 * half, electrons, orbitals), jnp.float32),
            pltpu.VMEM((2 * half, electrons, electrons), jnp.float32),
            pltpu.VMEM((2 * half, electrons, electrons), jnp.float32),
        ],
    )
    summed = lax.psum(density, "chip")
    return lax.all_gather(summed, "core", axis=0, tiled=True)


def solution(mesh):
    sections, walks = mesh.devices.shape
    split_mesh = Mesh(
        mesh.devices.reshape(sections // 2, 2, walks), ("chip", "core", "walk")
    )
    section = ("chip", "core")
    in_specs = (
        P(section, None, "walk"),
        P("walk", None, None),
        P(),
        P(section, "walk", None, None),
    )
    out_specs = P("walk", None, None)
    return jax.shard_map(
        body, mesh=split_mesh, in_specs=in_specs, out_specs=out_specs, check_vma=False
    )
```

time: 453 us -> 225 us (0.50)
  waiting for transfers between devices: 241 us -> 152 us
  other arithmetic: 70.1 us -> 0.21 us
  matrix products: 63.1 us -> 0 us
  local copies, waits for them, and re-layouts: 61.3 us -> 6.88 us
  Pallas kernels: 0 us -> 45.6 us
    another operation x7 -> x1, other arithmetic: 67.9 us -> 0.07 us  [body(): place = jnp.stack([chip, core]).astype(jnp.int32)]
    dot_general x30 -> x0, matrix products: 61.5 us -> none  [the longest x16 33.2 us: compose(): return jnp.einsum('wij,wjk->wik', later, earlier, precision=exact_mode)]
    reshape x1, local copies, waits for them, and re-layouts: 57.5 us -> 1.16 us  [contract(): field = jnp.repeat(jnp.transpose(field, (2, 0, 1)), PACK, axis=2)]
    unnamed x4 -> x2, waiting for transfers between devices: 46.8 us -> 0.03 us
    pallas_call x0 -> x4, Pallas kernels: none -> 45.6 us  [the longest x1 27.1 us: contract(): pl.pallas_call(functools.partial(contract_kernel, orbitals), grid=(blocks...]
    all_gather x1, waiting for transfers between devices: 104 us -> 61.4 us  [body(): everything = lax.all_gather(pair, 'chip')]
    ppermute x0 -> x3, waiting for transfers between devices: none -> 21.1 us  [the longest x1 18.2 us: body(): lax.ppermute(owned((walk + shift) % walk_size), 'walk', ring)]
    psum x1, waiting for transfers between devices: 90.3 us -> 69.7 us  [body(): summed = lax.psum(density, 'chip')]
  transfers between devices with their start and end apart: 3 -> 5, of which waited for: 3 -> 5; matrix products, arithmetic and copies ran while one was open for 0% -> 0% of each run, Pallas kernels for 0% -> 0%
where the time goes in v1:
time: 225 us; the launch traced here: 224 us
  waiting for transfers between devices  152 us (68%)
  Pallas kernels  45.6 us (20%)
  between operations  13.5 us (6%)
  local copies, waits for them, and re-layouts  6.88 us (3%)
  starting transfers between devices  3.35 us (1%)
  blocking collectives  2.59 us (1%)
    psum x1, waiting for transfers between devices, body(): summed = lax.psum(density, 'chip')  69.7 us
    all_gather x1, waiting for transfers between devices, body(): everything = lax.all_gather(pair, 'chip')  61.4 us
    pallas_call x1, Pallas kernels, contract(): pl.pallas_call(functools.partial(contract_kernel, orbitals), grid=(blocks...  27.1 us
    pallas_call x3, Pallas kernels, call(): pl.pallas_call(kernel, in_specs=[pl.BlockSpec(memory_space=pltpu.SMEM)] +...  18.4 us
    ppermute x1, waiting for transfers between devices, body(): lax.ppermute(owned((walk + shift) % walk_size), 'walk', ring)  18.2 us
  transfers between devices with their start and end apart: 5, of which 5 were waited for; matrix products, arithmetic and copies ran while one was open for 0% of the time, Pallas kernels for 0%

profile of v1, /device:TPU:0, one launch (start us, length us, event | category | flops | bytes accessed | tf_op | source)
XLA Modules:
  0.0 224.4 jit_solution(1379520373416403665)
XLA Ops:
  6.5 0.8 copy.10
  7.4 0.1 copy.11
  7.5 0.5 broadcast_in_dim.4
  8.0 1.2 reshape.14.field_ref
  9.1 27.1 %shard_map.46 = f32[8,200,200]{2,1,0:T(8,128)} custom-call(f32[2,8,3200]{2,1,0:T(8,128)} %reshape.14.field_ref, bf16[200,25,16,200]{3,2,1,0:T(8,128)(2,1)} %bitcast.15), custom_call_target="tpu_custom_call" | custom-call | tf_op jit(solution)/shard_map/pallas_call | solution.py:75
  36.2 1.3 constant_dynamic-slice_fusion.2
  37.6 3.0 %collective-permute-start = (f32[4,200,200]{2,1,0:T(8,128)S(1)}, f32[4,200,200]{2,1,0:T(8,128)S(1)}, u32[]{:S(2)}, u32[]{:S(2)}) collective-permute-start(f32[4,200,200]{2,1,0:T(8,128)S(1)} %constant_dynamic-slice_fusion.2), channel_id=1, source_target_pairs={{0,1},{1,0},{2,3},{3,2},{4,5},{5,4},{6,7},{7,6},{8,9},{9,8},{10,11... | collective-permute-start | bytes 1920008 | tf_op jit(solution)/shard_map/ppermute | solution.py:220
  40.6 0.1 pad_add_fusion.place_ref
  40.7 18.2 %collective-permute-done = f32[4,200,200]{2,1,0:T(8,128)S(1)} collective-permute-done((f32[4,200,200]{2,1,0:T(8,128)S(1)}, f32[4,200,200]{2,1,0:T(8,128)S(1)}, u32[]{:S(2)}, u32[]{:S(2)}) %collective-permute-start) | collective-permute-done | bytes 640032 | tf_op jit(solution)/shard_map/ppermute | solution.py:220
  58.8 0.1 dynamic-slice_add_fusion.field_ref
  59.0 2.7 %shard_map.47 = (f32[2,200,200]{2,1,0:T(8,128)S(1)}, f32[2,200,200]{2,1,0:T(8,128)S(1)}) custom-call(s32[2]{0:T(128)S(1)} %pad_add_fusion.place_ref, f32[4,200,200]{2,1,0:T(8,128)S(1)} %dynamic-slice_add_fusion.field_ref), custom_call_target="tpu_custom_call" | custom-call | tf_op jit(solution)/shard_map/pallas_call | solution.py:184
  61.7 0.1 collective-permute-start.1
  61.8 1.7 collective-permute-done.1.other_ref
  63.5 1.7 shard_map.48
  65.3 0.0 all-reduce.2.cloned.1.call-start
  65.4 0.2 collective-permute-start.2
  65.6 0.1 copy.12
  65.7 1.2 collective-permute-done.2.walk_other_ref
  66.9 61.4 %all-gather.3.cloned.1.call-done = f32[16,200,200]{2,1,0:T(8,128)} async-done(((f32[2,200,200]{2,1,0:T(8,128)}), f32[16,200,200]{2,1,0:T(8,128)}) %all-gather.3.cloned.1.call-update) | async-done | bytes 2560016 | tf_op jit(solution)/shard_map/all_gather | solution.py:228
  128.4 1.9 copy-done
  130.3 14.0 %shard_map.49 = f32[2,200,200]{2,1,0:T(8,128)} custom-call(s32[2]{0:T(128)S(1)} %pad_add_fusion.place_ref, f32[8,2,200,200]{3,2,1,0:T(8,128)S(1)} %bitcast.13, f32[2,200,200]{2,1,0:T(8,128)S(1)} %get-tuple-element.7.keep_ref, f32[2,200,200]{2,1,0:T(8,128)S(1)} %collective-permute-done.1.other_ref, f32[100,200]{1,0:T(8,128)S(1)} %bitcast.14, ...), custom_call_target="tpu_custom_call" | custom-call | tf_op jit(solution)/shard_map/pallas_call | solution.py:184
  144.3 69.7 %all-reduce.2.cloned.1.call-done = f32[2,200,200]{2,1,0:T(8,128)} async-done(((f32[2,200,200]{2,1,0:T(8,128)}), f32[2,200,200]{2,1,0:T(8,128)}) %all-reduce.2.cloned.1.call-update) | async-done | bytes 320016 | tf_op jit(solution)/shard_map/psum | solution.py:239
  214.1 2.6 %all_gather.11 = f32[4,200,200]{2,1,0:T(8,128)S(1)} all-gather(f32[2,200,200]{2,1,0:T(8,128)} %all-reduce.2.cloned.1.call-done), channel_id=1, replica_groups=mesh['chip'=8,'core'=2,'walk'=2] {'core'}, dimensions={0}, use_global_device_ids=true | all-gather | bytes 960000 | tf_op jit(solution)/shard_map/all_gather | solution.py:240
  216.6 0.9 copy.15
  (12 shorter events, 0.1 us)
Async XLA Ops:
  6.5 121.8 %all-gather.3.cloned.1.call-start = ((), (), s32[]{:S(2)}) async-start(), calls=%async_computation.1 | async-start | bytes 3686400 | tf_op jit(solution)/shard_map/all_gather | solution.py:228
  36.2 22.6 %copy-start.1 = (f32[8,200,200]{2,1,0:T(8,128)S(1)}, f32[8,200,200]{2,1,0:T(8,128)}, u32[]{:S(2)}) copy-start(f32[8,200,200]{2,1,0:T(8,128)} %shard_map.46) | copy-start | bytes 3840004
  37.6 21.3 %collective-permute-start = (f32[4,200,200]{2,1,0:T(8,128)S(1)}, f32[4,200,200]{2,1,0:T(8,128)S(1)}, u32[]{:S(2)}, u32[]{:S(2)}) collective-permute-start(f32[4,200,200]{2,1,0:T(8,128)S(1)} %constant_dynamic-slice_fusion.2), channel_id=1, source_target_pairs={{0,1},{1,0},{2,3},{3,2},{4,5},{5,4},{6,7},{7,6},{8,9},{9,8},{10,11... | collective-permute-start | bytes 1920008 | tf_op jit(solution)/shard_map/ppermute | solution.py:220
  59.0 6.4 %copy-start.2 = (f32[200,100]{1,0:T(8,128)S(1)}, f32[200,100]{1,0:T(8,128)}, u32[]{:S(2)}) copy-start(f32[200,100]{1,0:T(8,128)} %param.6) | copy-start | bytes 240004
  59.0 6.3 %copy-start.3 = (bf16[1,4,200,100]{3,2,1,0:T(8,128)(2,1)S(1)}, bf16[1,4,200,100]{3,2,1,0:T(8,128)(2,1)}, u32[]{:S(2)}) copy-start(bf16[1,4,200,100]{3,2,1,0:T(8,128)(2,1)} %param.7) | copy-start | bytes 480004
  61.7 1.8 collective-permute-start.1
  65.3 148.8 %all-reduce.2.cloned.1.call-start = ((), (), s32[]{:S(2)}) async-start(), calls=%async_computation | async-start | bytes 819200 | tf_op jit(solution)/shard_map/psum | solution.py:239
  65.4 1.5 collective-permute-start.2
  128.4 1.9 copy-start
Sparse Core Ops, SparseCore 0:
  65.4 62.9 all-gather.2
  144.5 69.5 all-reduce.1
